TPU v7x, 256 devices: a whole 4x4x8 slice. The times are simulated.
256 devices in a mesh: grp: 8 (over z), mem: 32 (over y, x, core).
Axes of the slice: x: 4, y: 4, z: 8, core: 2. Of those that a mesh axis runs over, the one named last changes fastest.
Arguments:
- child_means: float32 [524288, 64], P(('grp', 'mem')), may hold values from -48 to 48
- child_variances: float32 [524288, 64], P(('grp', 'mem')), may hold values from 0.2 to 2
- virtual_counts: int32 [524288], P(('grp', 'mem')), may hold values from 1 to 4
- assignment: int32 [524288, 1], P(('grp', 'mem')), may hold values from 0 to 511
Outputs:
- parent_means: float32 [512, 64], P('mem')
- parent_variances: float32 [512, 64], P('mem')
- parent_weights: float32 [512], P('mem')
All inputs are finite; a program needn't handle non-finite values.
Results may differ from a plain program's by a relative error of at most 0.0003.
Values sent between devices are 32-bit elements; how exact they have to be, the bound alone decides.
No kernel may reach another device: no remote copies, remote signals or barrier semaphores. Data moves between devices by JAX's collectives and lax.ppermute only.
A program may use at most 64 MiB of HBM per device.

v0:
```python
import math
import jax
import jax.numpy as jnp
from jax import lax
from jax.sharding import Mesh
from jax.sharding import PartitionSpec as P

P_SIZE = 512
ITERS = 2
GRP_MEM = ("grp", "mem_0", "mem_1", "mem_2")
MEM = ("mem_0", "mem_1", "mem_2")


def by_axis(value, axes):
    for axis in axes:
        value = lax.psum(value, axis)
    return value


def cut_along(value, dim, size):
    before, after = (value.shape[:dim], value.shape[dim + 1 :])
    return jnp.moveaxis(value.reshape(*before, size, -1, *after), dim, 0)


def summed_on_arrival(value, axis, dim):
    size = lax.axis_size(axis)
    pieces = lax.all_to_all(cut_along(value, dim, size), axis, 0, 0, tiled=True)
    return jnp.sum(pieces, axis=0)


def in_one_piece(arrays, axis, dim, along):
    columns = [a.reshape(*a.shape[:along], -1) for a in arrays]
    both = jnp.concatenate(columns, axis=along)
    filled, at, done = (summed_on_arrival(both, axis, dim), 0, [])
    for a, column in zip(arrays, columns):
        section = filled[..., at : at + column.shape[along]]
        done.append(section.reshape(*section.shape[:along], *a.shape[along:]))
        at += column.shape[along]
    return tuple(done)


def copy_for_each(value, axis):
    size = lax.axis_size(axis)
    return lax.all_to_all(
        jnp.broadcast_to(value[None], (size, *value.shape)), axis, 0, 0, tiled=True
    )


def taken_together(value, axis):
    return copy_for_each(value, axis).sum(axis=0)


def in_one(arrays, axis):
    ends = [0]
    for a in arrays:
        ends.append(ends[-1] + a.size)
    total = taken_together(jnp.concatenate([a.ravel() for a in arrays]), axis)
    return tuple((total[b:e].reshape(a.shape) for a, b, e in zip(arrays, ends, ends[1:])))


def in_one_piece_2(arrays, axis, dim, along):
    columns = [a.reshape(*a.shape[:along], -1) for a in arrays]
    both = jnp.concatenate(columns, axis=along)
    filled, at, done = (lax.all_gather(both, axis, axis=dim, tiled=True), 0, [])
    for a, column in zip(arrays, columns):
        section = filled[..., at : at + column.shape[along]]
        done.append(section.reshape(*section.shape[:along], *a.shape[along:]))
        at += column.shape[along]
    return tuple(done)


def child_features(means, variances):
    return jnp.concatenate([means, variances + means * means], axis=1)


def accumulate(features, extras, weigh):
    row_count = features.shape[0]
    block = math.gcd(row_count, 1024)
    turns = row_count // block
    pieces = (features.reshape(turns, block, features.shape[1]),) + tuple(
        (extra.reshape((turns, block) + extra.shape[1:]) for extra in extras)
    )

    def advance(carry, piece):
        weights = weigh(*piece)
        sums = carry[0] + lax.dot_general(
            weights,
            piece[0],
            (((0,), (0,)), ((), ())),
            precision=lax.Precision.HIGHEST,
            preferred_element_type=jnp.float32,
        )
        counts = carry[1] + jnp.sum(weights, axis=0)
        return ((sums, counts), None)

    start_sums = (
        jnp.zeros((P_SIZE, features.shape[1]), jnp.float32),
        jnp.zeros((P_SIZE,), jnp.float32),
    )
    return lax.scan(advance, start_sums, pieces)[0]


def maximize(counts, sums, total):
    width = sums.shape[1] // 2
    mass = counts + 1.0
    means = sums[:, :width] / mass[:, None]
    second = (sums[:, width:] + 1.0) / mass[:, None]
    return (means, second - means * means, mass / (total + P_SIZE))


def parent_table(means, variances, weights):
    inverse = 1.0 / variances
    table = jnp.concatenate([-2.0 * means * inverse, inverse], axis=1)
    offset = jnp.sum(jnp.log(2.0 * math.pi * variances) + means * means * inverse, axis=1)
    return (table, offset, jnp.log(weights))


def soft_weights(block_features, block_virtual, table, offset, log_weight):
    width = block_features.shape[1] // 2
    cross = lax.dot_general(
        block_features,
        table,
        (((1,), (1,)), ((), ())),
        precision=lax.Precision.HIGHEST,
        preferred_element_type=jnp.float32,
    )
    ell = -0.5 / width * (cross + offset[None, :])
    score = log_weight[None, :] + block_virtual[:, None] * ell
    top = jnp.max(score, axis=1, keepdims=True)
    expd = jnp.exp(score - top)
    resp = expd / jnp.sum(expd, axis=1, keepdims=True)
    return resp * block_virtual[:, None]


def shards(child_means, child_variances, virtual_counts, assignment):
    features = child_features(child_means, child_variances)
    virtual = virtual_counts.astype(jnp.float32)
    labels = jnp.arange(P_SIZE, dtype=jnp.int32)

    def initial_weights(block_features, block_virtual, block_assign):
        return (block_assign == labels[None, :]).astype(jnp.float32) * block_virtual[:, None]

    sums, counts = accumulate(features, (virtual, assignment), initial_weights)
    total = by_axis(jnp.sum(virtual), GRP_MEM)

    def combine(local_sums, local_counts):
        shared = in_one_piece((local_sums, local_counts), MEM, 0, 1)
        return in_one((shared[0], shared[1]), "grp")

    own_sums, own_counts = combine(sums, counts)
    means, variances, weights = maximize(own_counts, own_sums, total)
    for iteration in range(ITERS):
        all_means, all_variances, all_weights = in_one_piece_2(
            (means, variances, weights), MEM, 0, 1
        )
        table, offset, log_weight = parent_table(all_means, all_variances, all_weights)

        def weigh(block_features, block_virtual):
            return soft_weights(block_features, block_virtual, table, offset, log_weight)

        sums, counts = accumulate(features, (virtual,), weigh)
        own_sums, own_counts = combine(sums, counts)
        means, variances, weights = maximize(own_counts, own_sums, total)
    return (means, variances, weights)


def solution(mesh):
    split = Mesh(
        mesh.devices.reshape(mesh.shape["grp"], 4, 4, 2), ("grp", "mem_0", "mem_1", "mem_2")
    )
    return jax.shard_map(
        shards,
        mesh=split,
        in_specs=(P(GRP_MEM, None), P(GRP_MEM, None), P(GRP_MEM), P(GRP_MEM, None)),
        out_specs=(P(MEM, None), P(MEM, None), P(MEM)),
        check_vma=False,
    )
```

profile of v0, /device:TPU:1, one launch (start us, length us, event | category | flops | bytes accessed | tf_op | source)
XLA Modules:
  0.0 213.9 jit_solution(10653394932134514791)
XLA Ops:
  0.6 1.3 multiply_add_fusion.2
  1.9 1.2 pad_maximum_fusion
  3.1 0.3 copy.28
  3.5 8.4 %while.39 = (s32[]{:T(128)}, f32[512,128]{1,0:T(8,128)S(1)}, f32[512]{0:T(512)S(1)}, s32[2,1024,1]{1,2,0:T(1,128)S(1)}, f32[2,1024]{1,0:T(2,128)S(1)}, /*index=5*/f32[2,1024,128]{2,1,0:T(8,128)S(1)}, s32[]{:T(128)}, s32[]{:T(128)}) while((s32[]{:T(128)}, f32[512,128]{1,0:T(8,128)S(1)}, f32[512]{0:T(512)S(1)}, ...), condition=%wide.region_2.3_spmd.clone, body=%wide.region_0.2_spmd.clone.sunk | while | flops 808059392 | bytes 1089644 | solution.py:100
  3.5 3.8 %fusion.57 = f32[512,128]{1,0:T(8,128)S(1)} fusion(f32[1024]{0:T(1024)S(1)} %bitcast.73, s32[1024]{0:T(1024)S(1)} %bitcast.75, f32[2,1024,128]{2,1,0:T(8,128)S(1)} %get-tuple-element.440, s32[]{:T(128)} %get-tuple-element.427, f32[512,128]{1,0:T(8,128)S(1)} %get-tuple-element.428, pred[]{:T(512)S(6)} %compare.9), kind=kOutput, calls=%fused_computation.5.clone.1 | convolution fusion | flops 806486016 | bytes 1056773 | tf_op jit(solution)/shard_map/while/body/eval_jaxpr/dot_general | solution.py:86
  7.3 0.3 select_reduce_fusion.2
  7.7 3.8 %fusion.57 = f32[512,128]{1,0:T(8,128)S(1)} fusion(f32[1024]{0:T(1024)S(1)} %bitcast.73, s32[1024]{0:T(1024)S(1)} %bitcast.75, f32[2,1024,128]{2,1,0:T(8,128)S(1)} %get-tuple-element.440, s32[]{:T(128)} %get-tuple-element.427, f32[512,128]{1,0:T(8,128)S(1)} %get-tuple-element.428, pred[]{:T(512)S(6)} %compare.9), kind=kOutput, calls=%fused_computation.5.clone.1 | convolution fusion | flops 806486016 | bytes 1056773 | tf_op jit(solution)/shard_map/while/body/eval_jaxpr/dot_general | solution.py:86
  11.5 0.3 select_reduce_fusion.2
  11.9 0.2 concatenate.65
  12.1 19.8 %all_to_all.33 = f32[32,16,129]{2,1,0:T(8,128)S(1)} all-to-all(f32[32,16,129]{2,1,0:T(8,128)S(1)} %pad_maximum_fusion.1), channel_id=1, replica_groups=mesh['grp'=8,'mem_0'=4,'mem_1'=4,'mem_2'=2] {'mem_0','mem_1','mem_2'}, dimensions={0} | all-to-all | bytes 528384 | tf_op jit(solution)/shard_map/all_to_all | solution.py:27
  32.0 0.1 slice_reduce_fusion.2
  32.1 0.7 broadcast_in_dim.8
  32.8 8.2 %all-to-all-start.1 = ((f32[8,1,2064]{2,1,0:T(1,128)}), f32[8,1,2064]{2,1,0:T(1,128)S(1)}, u32[]{:S(2)}, u32[]{:S(2)}) async-start(f32[8,1,2064]{2,1,0:T(1,128)} %broadcast_in_dim.8), calls=%async_computation.1 | async-start | bytes 139264 | tf_op jit(solution)/shard_map/all_to_all | solution.py:44
  41.0 0.6 convert_reduce_fusion
  41.6 14.2 %psum.28 = f32[]{:T(128)} all-reduce(f32[]{:T(128)} %convert_reduce_fusion), channel_id=1, replica_groups=mesh['grp'=8,'mem_0'=4,'mem_1'=4,'mem_2'=2] {'grp'}, use_global_device_ids=true, to_apply=%region_6.7 | all-reduce | flops 1 | bytes 8 | tf_op jit(solution)/shard_map/psum | solution.py:16
  55.8 7.2 %psum.29 = f32[]{:T(128)} all-reduce(f32[]{:T(128)} %psum.28), channel_id=1, replica_groups=mesh['grp'=8,'mem_0'=4,'mem_1'=4,'mem_2'=2] {'mem_0'}, use_global_device_ids=true, to_apply=%region_7.8 | all-reduce | flops 1 | bytes 8 | tf_op jit(solution)/shard_map/psum | solution.py:16
  63.0 8.1 %psum.30 = f32[]{:T(128)} all-reduce(f32[]{:T(128)} %psum.29), channel_id=1, replica_groups=mesh['grp'=8,'mem_0'=4,'mem_1'=4,'mem_2'=2] {'mem_1'}, use_global_device_ids=true, to_apply=%region_8.9 | all-reduce | flops 1 | bytes 8 | tf_op jit(solution)/shard_map/psum | solution.py:16
  71.0 10.5 %psum.31 = f32[]{:T(128)} all-reduce(f32[]{:T(128)} %psum.30), channel_id=1, replica_groups=mesh['grp'=8,'mem_0'=4,'mem_1'=4,'mem_2'=2] {'mem_2'}, use_global_device_ids=true, to_apply=%region_9.10 | all-reduce | flops 1 | bytes 8 | tf_op jit(solution)/shard_map/psum | solution.py:16
  82.3 0.1 copy.31
  82.4 0.1 slice_divide_fusion.4
  82.5 0.1 pad_maximum_fusion.6
  82.6 23.0 %all_gather.6 = f32[512,129]{1,0:T(8,128)S(1)} all-gather(f32[16,129]{1,0:T(8,128)S(1)} %pad_maximum_fusion.6), channel_id=1, replica_groups=mesh['grp'=8,'mem_0'=4,'mem_1'=4,'mem_2'=2] {'mem_0','mem_1','mem_2'}, dimensions={0}, use_global_device_ids=true | all-gather | bytes 272448 | tf_op jit(solution)/shard_map/all_gather | solution.py:64
  105.5 0.2 add_reduce_fusion.1
  105.8 0.2 fusion.31
  105.9 0.1 pad_maximum_fusion.4
  106.1 12.3 %while.40 = (s32[]{:T(128)}, f32[512,128]{1,0:T(8,128)}, f32[512]{0:T(512)S(1)}, f32[512]{0:T(512)S(1)}, f32[2,1024,128]{2,1,0:T(8,128)S(1)}, /*index=5*/f32[512...) while((s32[]{:T(128)}, f32[512,128]{1,0:T(8,128)}, ...), condition=%wide.region_15.16_spmd.clone, body=%wide.region_11.15_spmd.clone.sunk | while | flops 1617559040 | bytes 10293372 | solution.py:100
  106.1 2.0 fusion.60
  108.2 0.3 fusion.61
  108.5 0.5 fusion.62
  109.0 2.7 %convolution_add_fusion.4 = f32[512,128]{1,0:T(8,128)} fusion(f32[2,1024,128]{2,1,0:T(8,128)S(1)} %get-tuple-element.467, s32[]{:T(128)} %get-tuple-element.453, f32[1024,512]{0,1:T(8,128)S(1)} %get-tuple-element.407, f32[1024]{0:T(1024)S(1)} %bitcast.69, f32[1024]{0:T(1024)S(1)} %fusion.61, f32[1024]{0:T(1024)S(1)} %get-tuple-element.408, ...), kind=kOutput, calls=%fused_computation.20.clone.1 | convolution fusion | flops 807010304 | bytes 3158021 | tf_op jit(solution)/shard_map/while/body/eval_jaxpr/dot_general | solution.py:86
  111.8 2.0 fusion.60
  113.8 0.3 fusion.61
  114.2 0.5 fusion.62
  114.7 3.7 %convolution_add_fusion.4 = f32[512,128]{1,0:T(8,128)} fusion(f32[2,1024,128]{2,1,0:T(8,128)S(1)} %get-tuple-element.467, s32[]{:T(128)} %get-tuple-element.453, f32[1024,512]{0,1:T(8,128)S(1)} %get-tuple-element.407, f32[1024]{0:T(1024)S(1)} %bitcast.69, f32[1024]{0:T(1024)S(1)} %fusion.61, f32[1024]{0:T(1024)S(1)} %get-tuple-element.408, ...), kind=kOutput, calls=%fused_computation.20.clone.1 | convolution fusion | flops 807010304 | bytes 3158021 | tf_op jit(solution)/shard_map/while/body/eval_jaxpr/dot_general | solution.py:86
  118.3 0.2 concatenate.66
  118.5 1.0 pad_maximum_fusion.2
  119.5 16.1 %all_to_all.34 = f32[32,16,129]{2,1,0:T(8,128)S(1)} all-to-all(f32[32,16,129]{2,1,0:T(8,128)S(1)} %pad_maximum_fusion.2), channel_id=1, replica_groups=mesh['grp'=8,'mem_0'=4,'mem_1'=4,'mem_2'=2] {'mem_0','mem_1','mem_2'}, dimensions={0} | all-to-all | bytes 528384 | tf_op jit(solution)/shard_map/all_to_all | solution.py:27
  135.7 0.1 slice_reduce_fusion.1
  135.8 0.7 broadcast_in_dim.9
  136.5 4.3 %all-to-all-start.3 = ((f32[8,1,2064]{2,1,0:T(1,128)}), f32[8,1,2064]{2,1,0:T(1,128)S(1)}, u32[]{:S(2)}, u32[]{:S(2)}) async-start(f32[8,1,2064]{2,1,0:T(1,128)} %broadcast_in_dim.9), calls=%async_computation.3 | async-start | bytes 139264 | tf_op jit(solution)/shard_map/all_to_all | solution.py:44
  140.7 7.2 %all-to-all-done.3 = f32[8,1,2064]{2,1,0:T(1,128)S(1)} async-done(((f32[8,1,2064]{2,1,0:T(1,128)}), f32[8,1,2064]{2,1,0:T(1,128)S(1)}, u32[]{:S(2)}, u32[]{:S(2)}) %all-to-all-start.3) | async-done | bytes 66080 | tf_op jit(solution)/shard_map/all_to_all | solution.py:44
  148.0 0.1 copy.34
  148.1 0.1 slice_divide_fusion.3
  148.2 0.1 pad_maximum_fusion.7
  148.2 24.9 %all_gather.7 = f32[512,129]{1,0:T(8,128)S(1)} all-gather(f32[16,129]{1,0:T(8,128)S(1)} %pad_maximum_fusion.7), channel_id=1, replica_groups=mesh['grp'=8,'mem_0'=4,'mem_1'=4,'mem_2'=2] {'mem_0','mem_1','mem_2'}, dimensions={0}, use_global_device_ids=true | all-gather | bytes 272448 | tf_op jit(solution)/shard_map/all_gather | solution.py:64
  173.2 0.2 add_reduce_fusion
  173.4 0.2 fusion.30
  173.6 0.1 pad_maximum_fusion.5
  173.7 12.3 %while.41 = (s32[]{:T(128)}, f32[512,128]{1,0:T(8,128)}, f32[512]{0:T(512)S(1)}, f32[512]{0:T(512)S(1)}, f32[2,1024,128]{2,1,0:T(8,128)S(1)}, /*index=5*/f32[512...) while((s32[]{:T(128)}, f32[512,128]{1,0:T(8,128)}, ...), condition=%wide.region_23.24_spmd.clone, body=%wide.region_19.23_spmd.clone.sunk | while | flops 1617559040 | bytes 10293372 | solution.py:100
  173.8 2.0 fusion.65
  175.8 0.3 fusion.66
  176.2 0.5 fusion.67
  176.7 2.7 %convolution_add_fusion.5 = f32[512,128]{1,0:T(8,128)} fusion(f32[2,1024,128]{2,1,0:T(8,128)S(1)} %get-tuple-element.497, s32[]{:T(128)} %get-tuple-element.483, f32[1024,512]{0,1:T(8,128)S(1)} %get-tuple-element.417, f32[1024]{0:T(1024)S(1)} %bitcast.72, f32[1024]{0:T(1024)S(1)} %fusion.66, f32[1024]{0:T(1024)S(1)} %get-tuple-element.418, ...), kind=kOutput, calls=%fused_computation.35.clone.1 | convolution fusion | flops 807010304 | bytes 3158021 | tf_op jit(solution)/shard_map/while/body/eval_jaxpr/dot_general | solution.py:86
  179.4 2.0 fusion.65
  181.5 0.3 fusion.66
  181.8 0.5 fusion.67
  182.3 3.7 %convolution_add_fusion.5 = f32[512,128]{1,0:T(8,128)} fusion(f32[2,1024,128]{2,1,0:T(8,128)S(1)} %get-tuple-element.497, s32[]{:T(128)} %get-tuple-element.483, f32[1024,512]{0,1:T(8,128)S(1)} %get-tuple-element.417, f32[1024]{0:T(1024)S(1)} %bitcast.72, f32[1024]{0:T(1024)S(1)} %fusion.66, f32[1024]{0:T(1024)S(1)} %get-tuple-element.418, ...), kind=kOutput, calls=%fused_computation.35.clone.1 | convolution fusion | flops 807010304 | bytes 3158021 | tf_op jit(solution)/shard_map/while/body/eval_jaxpr/dot_general | solution.py:86
  186.0 0.2 concatenate.67
  186.2 1.0 pad_maximum_fusion.3
  187.2 15.7 %all_to_all.35 = f32[32,16,129]{2,1,0:T(8,128)S(1)} all-to-all(f32[32,16,129]{2,1,0:T(8,128)S(1)} %pad_maximum_fusion.3), channel_id=1, replica_groups=mesh['grp'=8,'mem_0'=4,'mem_1'=4,'mem_2'=2] {'mem_0','mem_1','mem_2'}, dimensions={0} | all-to-all | bytes 528384 | tf_op jit(solution)/shard_map/all_to_all | solution.py:27
  202.9 0.1 slice_reduce_fusion
  203.1 9.6 %all_to_all.36 = f32[8,1,2064]{2,1,0:T(1,128)S(1)} all-to-all(f32[8,1,2064]{2,1,0:T(1,128)S(1)} %broadcast_in_dim.10), channel_id=1, replica_groups=mesh['grp'=8,'mem_0'=4,'mem_1'=4,'mem_2'=2] {'grp'}, dimensions={0} | all-to-all | bytes 132096 | tf_op jit(solution)/shard_map/all_to_all | solution.py:44
  212.7 0.5 broadcast_divide_fusion
  213.3 0.7 fusion.33
  (50 shorter events, 0.7 us)
Async XLA Ops:
  1.9 1.5 copy-start.1
  1.9 1.5 copy-start
  32.8 49.4 %all-to-all-start.1 = ((f32[8,1,2064]{2,1,0:T(1,128)}), f32[8,1,2064]{2,1,0:T(1,128)S(1)}, u32[]{:S(2)}, u32[]{:S(2)}) async-start(f32[8,1,2064]{2,1,0:T(1,128)} %broadcast_in_dim.8), calls=%async_computation.1 | async-start | bytes 139264 | tf_op jit(solution)/shard_map/all_to_all | solution.py:44
  136.5 11.5 %all-to-all-start.3 = ((f32[8,1,2064]{2,1,0:T(1,128)}), f32[8,1,2064]{2,1,0:T(1,128)S(1)}, u32[]{:S(2)}, u32[]{:S(2)}) async-start(f32[8,1,2064]{2,1,0:T(1,128)} %broadcast_in_dim.9), calls=%async_computation.3 | async-start | bytes 139264 | tf_op jit(solution)/shard_map/all_to_all | solution.py:44
where the time goes:
time: 215 us; the launch traced here: 214 us
  blocking collectives  149 us (69%)
  matrix products  28.5 us (13%)
  starting transfers between devices  12.4 us (6%)
  other arithmetic  11.8 us (5%)
  waiting for transfers between devices  7.2 us (3%)
  local copies, waits for them, and re-layouts  3.24 us (2%)
    all_to_all x3, blocking collectives, summed_on_arrival(): pieces = lax.all_to_all(cut_along(value, dim, size), axis, 0, 0, tiled=True)  51.6 us
    all_gather x2, blocking collectives, in_one_piece_2(): filled, at, done = (lax.all_gather(both, axis, axis=dim, tiled=True), 0, [])  47.9 us
    psum x4, blocking collectives, by_axis(): value = lax.psum(value, axis)  40 us
    dot_general x6, matrix products, advance(): lax.dot_general(weights, piece[0], (((0,), (0,)), ((), ())), precision=la...  20.3 us
    all_to_all x2, starting transfers between devices, copy_for_each(): lax.all_to_all(jnp.broadcast_to(value[None], (size, *value.shape)), axis,...  12.4 us
    all_to_all x1, blocking collectives, copy_for_each(): lax.all_to_all(jnp.broadcast_to(value[None], (size, *value.shape)), axis,...  9.55 us
    dot_general x4, matrix products, soft_weights(): lax.dot_general(block_features, table, (((1,), (1,)), ((), ())), precisio...  8.19 us
    all_to_all x2, waiting for transfers between devices, copy_for_each(): lax.all_to_all(jnp.broadcast_to(value[None], (size, *value.shape)), axis,...  7.2 us
  transfers between devices with their start and end apart: 2, of which 1 were waited for; matrix products, arithmetic and copies ran while one was open for 0% of the time, Pallas kernels for 0%

commit v1 on v0

--- a/solution.py
+++ b/solution.py
@@ -13,7 +13,8 @@
 
 def by_axis(value, axes):
     for axis in axes:
-        value = lax.psum(value, axis)
+        terms = lax.all_gather(value, axis)
+        value = jnp.sum(terms, axis=0)
     return value
 
 

time: 215 us -> 224 us (1.042)
  blocking collectives: 149 us -> 127 us
  waiting for transfers between devices: 7.2 us -> 18.6 us
  starting transfers between devices: 12.4 us -> 21 us
  local copies, waits for them, and re-layouts: 3.24 us -> 11.2 us
  other arithmetic: 11.8 us -> 15 us
    psum x4 -> x0, blocking collectives: 40 us -> none  [by_axis(): value = lax.psum(value, axis)]
    unnamed x0 -> x4, blocking collectives: none -> 37.5 us
    all_to_all x3 -> x2, blocking collectives: 51.6 us -> 31.7 us  [summed_on_arrival(): pieces = lax.all_to_all(cut_along(value, dim, size), axis, 0, 0, tiled=True)]
    all_to_all x0 -> x1, waiting for transfers between devices: none -> 11.4 us  [summed_on_arrival(): pieces = lax.all_to_all(cut_along(value, dim, size), axis, 0, 0, tiled=True)]
    all_to_all x0 -> x1, starting transfers between devices: none -> 8.58 us  [summed_on_arrival(): pieces = lax.all_to_all(cut_along(value, dim, size), axis, 0, 0, tiled=True)]
    unnamed x4 -> x24, local copies, waits for them, and re-layouts: 0.01 us -> 7.98 us
    reduce_sum x0 -> x4, other arithmetic: none -> 2.4 us  [by_axis(): value = jnp.sum(terms, axis=0)]
  transfers between devices with their start and end apart: 2 -> 3, of which waited for: 1 -> 2; matrix products, arithmetic and copies ran while one was open for 0% -> 5% of each run, Pallas kernels for 0% -> 0%
where the time goes in v1:
time: 224 us; the launch traced here: 223 us
  blocking collectives  127 us (57%)
  matrix products  28.5 us (13%)
  starting transfers between devices  21 us (9%)
  waiting for transfers between devices  18.6 us (8%)
  other arithmetic  15 us (7%)
  local copies, waits for them, and re-layouts  11.2 us (5%)
    all_gather x2, blocking collectives, in_one_piece_2(): filled, at, done = (lax.all_gather(both, axis, axis=dim, tiled=True), 0, [])  47.9 us
    unnamed x4, blocking collectives  37.5 us
    all_to_all x2, blocking collectives, summed_on_arrival(): pieces = lax.all_to_all(cut_along(value, dim, size), axis, 0, 0, tiled=True)  31.7 us
    dot_general x6, matrix products, advance(): lax.dot_general(weights, piece[0], (((0,), (0,)), ((), ())), precision=la...  20.3 us
    all_to_all x2, starting transfers between devices, copy_for_each(): lax.all_to_all(jnp.broadcast_to(value[None], (size, *value.shape)), axis,...  12.4 us
    all_to_all x1, waiting for transfers between devices, summed_on_arrival(): pieces = lax.all_to_all(cut_along(value, dim, size), axis, 0, 0, tiled=True)  11.4 us
    all_to_all x1, blocking collectives, copy_for_each(): lax.all_to_all(jnp.broadcast_to(value[None], (size, *value.shape)), axis,...  9.55 us
    all_to_all x1, starting transfers between devices, summed_on_arrival(): pieces = lax.all_to_all(cut_along(value, dim, size), axis, 0, 0, tiled=True)  8.58 us
  transfers between devices with their start and end apart: 3, of which 2 were waited for; matrix products, arithmetic and copies ran while one was open for 5% of the time, Pallas kernels for 0%

profile of v1, /device:TPU:1, one launch (start us, length us, event | category | flops | bytes accessed | tf_op | source)
XLA Modules:
  0.0 222.8 jit_solution(2434122119322258617)
XLA Ops:
  0.6 1.3 multiply_add_fusion.2
  1.9 1.2 pad_maximum_fusion
  3.1 0.3 copy.28
  3.5 8.4 %while.39 = (s32[]{:T(128)}, f32[512,128]{1,0:T(8,128)S(1)}, f32[512]{0:T(512)S(1)}, s32[2,1024,1]{1,2,0:T(1,128)S(1)}, f32[2,1024]{1,0:T(2,128)S(1)}, /*index=5*/f32[2,1024,128]{2,1,0:T(8,128)S(1)}, s32[]{:T(128)}, s32[]{:T(128)}) while((s32[]{:T(128)}, f32[512,128]{1,0:T(8,128)S(1)}, f32[512]{0:T(512)S(1)}, ...), condition=%wide.region_2.3_spmd.clone, body=%wide.region_0.2_spmd.clone.sunk | while | flops 808059392 | bytes 1089644 | solution.py:101
  3.5 3.8 %fusion.57 = f32[512,128]{1,0:T(8,128)S(1)} fusion(f32[1024]{0:T(1024)S(1)} %bitcast.81, s32[1024]{0:T(1024)S(1)} %bitcast.83, f32[2,1024,128]{2,1,0:T(8,128)S(1)} %get-tuple-element.440, s32[]{:T(128)} %get-tuple-element.427, f32[512,128]{1,0:T(8,128)S(1)} %get-tuple-element.428, pred[]{:T(512)S(6)} %compare.9), kind=kOutput, calls=%fused_computation.5.clone.1 | convolution fusion | flops 806486016 | bytes 1056773 | tf_op jit(solution)/shard_map/while/body/eval_jaxpr/dot_general | solution.py:87
  7.3 0.3 select_reduce_fusion.2
  7.7 3.8 %fusion.57 = f32[512,128]{1,0:T(8,128)S(1)} fusion(f32[1024]{0:T(1024)S(1)} %bitcast.81, s32[1024]{0:T(1024)S(1)} %bitcast.83, f32[2,1024,128]{2,1,0:T(8,128)S(1)} %get-tuple-element.440, s32[]{:T(128)} %get-tuple-element.427, f32[512,128]{1,0:T(8,128)S(1)} %get-tuple-element.428, pred[]{:T(512)S(6)} %compare.9), kind=kOutput, calls=%fused_computation.5.clone.1 | convolution fusion | flops 806486016 | bytes 1056773 | tf_op jit(solution)/shard_map/while/body/eval_jaxpr/dot_general | solution.py:87
  11.5 0.3 select_reduce_fusion.2
  11.9 0.2 concatenate.65
  12.1 0.8 pad_maximum_fusion.1
  13.0 8.6 %all-to-all-start = ((f32[32,16,129]{2,1,0:T(8,128)}), f32[32,16,129]{2,1,0:T(8,128)S(1)}, u32[]{:S(2)}, u32[]{:S(2)}) async-start(f32[32,16,129]{2,1,0:T(8,128)} %pad_maximum_fusion.1), calls=%async_computation | async-start | bytes 1048576 | tf_op jit(solution)/shard_map/all_to_all | solution.py:28
  21.5 11.4 %all-to-all-done = f32[32,16,129]{2,1,0:T(8,128)S(1)} async-done(((f32[32,16,129]{2,1,0:T(8,128)}), f32[32,16,129]{2,1,0:T(8,128)S(1)}, u32[]{:S(2)}, u32[]{:S(2)}) %all-to-all-start) | async-done | bytes 264224 | tf_op jit(solution)/shard_map/all_to_all | solution.py:28
  33.2 0.7 broadcast_in_dim.8
  33.8 8.2 %all-to-all-start.1 = ((f32[8,1,2064]{2,1,0:T(1,128)}), f32[8,1,2064]{2,1,0:T(1,128)S(1)}, u32[]{:S(2)}, u32[]{:S(2)}) async-start(f32[8,1,2064]{2,1,0:T(1,128)} %broadcast_in_dim.8), calls=%async_computation.1 | async-start | bytes 139264 | tf_op jit(solution)/shard_map/all_to_all | solution.py:45
  42.0 0.6 dynamic-slice
  42.6 0.6 convert_reduce_fusion
  43.2 1.4 dynamic-update-slice
  44.6 13.4 %all-reduce = f32[8]{0:T(128)S(1)} all-reduce(f32[8]{0:T(128)S(1)} %dynamic-update-slice), channel_id=1, replica_groups=mesh['grp'=8,'mem_0'=4,'mem_1'=4,'mem_2'=2] {'grp'}, use_global_device_ids=true, to_apply=%add | all-reduce | flops 8 | bytes 64
  58.0 0.6 dynamic-slice.1
  58.6 0.6 reduce_sum.165
  59.2 1.4 dynamic-update-slice.1
  60.6 6.7 %all-reduce.1 = f32[4]{0:T(128)S(1)} all-reduce(f32[4]{0:T(128)S(1)} %dynamic-update-slice.1), channel_id=1, replica_groups=mesh['grp'=8,'mem_0'=4,'mem_1'=4,'mem_2'=2] {'mem_0'}, use_global_device_ids=true, to_apply=%add.1 | all-reduce | flops 4 | bytes 32
  67.3 0.6 dynamic-slice.2
  67.9 0.6 reduce_sum.166
  68.5 1.4 dynamic-update-slice.2
  69.9 7.4 %all-reduce.2 = f32[4]{0:T(128)S(1)} all-reduce(f32[4]{0:T(128)S(1)} %dynamic-update-slice.2), channel_id=1, replica_groups=mesh['grp'=8,'mem_0'=4,'mem_1'=4,'mem_2'=2] {'mem_1'}, use_global_device_ids=true, to_apply=%add.2 | all-reduce | flops 4 | bytes 32
  77.3 0.6 dynamic-slice.3
  77.9 0.6 reduce_sum.167
  78.5 1.4 dynamic-update-slice.3
  79.9 9.9 %all-reduce.3 = f32[2]{0:T(128)S(1)} all-reduce(f32[2]{0:T(128)S(1)} %dynamic-update-slice.3), channel_id=1, replica_groups=mesh['grp'=8,'mem_0'=4,'mem_1'=4,'mem_2'=2] {'mem_2'}, use_global_device_ids=true, to_apply=%add.3 | all-reduce | flops 2 | bytes 16
  89.8 0.6 reduce_sum.168
  91.4 23.0 %all_gather.38 = f32[512,129]{1,0:T(8,128)S(1)} all-gather(f32[16,129]{1,0:T(8,128)S(1)} %pad_maximum_fusion.6), channel_id=1, replica_groups=mesh['grp'=8,'mem_0'=4,'mem_1'=4,'mem_2'=2] {'mem_0','mem_1','mem_2'}, dimensions={0}, use_global_device_ids=true | all-gather | bytes 272448 | tf_op jit(solution)/shard_map/all_gather | solution.py:65
  114.4 0.2 add_reduce_fusion.1
  115.0 12.3 %while.40 = (s32[]{:T(128)}, f32[512,128]{1,0:T(8,128)}, f32[512]{0:T(512)S(1)}, f32[512]{0:T(512)S(1)}, f32[2,1024,128]{2,1,0:T(8,128)S(1)}, /*index=5*/f32[512...) while((s32[]{:T(128)}, f32[512,128]{1,0:T(8,128)}, ...), condition=%wide.region_15.16_spmd.clone, body=%wide.region_11.15_spmd.clone.sunk | while | flops 1617559040 | bytes 10293372 | solution.py:101
  115.0 2.0 fusion.60
  117.0 0.3 fusion.61
  117.4 0.5 fusion.62
  117.9 2.7 %convolution_add_fusion.4 = f32[512,128]{1,0:T(8,128)} fusion(f32[2,1024,128]{2,1,0:T(8,128)S(1)} %get-tuple-element.467, s32[]{:T(128)} %get-tuple-element.453, f32[1024,512]{0,1:T(8,128)S(1)} %get-tuple-element.407, f32[1024]{0:T(1024)S(1)} %bitcast.77, f32[1024]{0:T(1024)S(1)} %fusion.61, f32[1024]{0:T(1024)S(1)} %get-tuple-element.408, ...), kind=kOutput, calls=%fused_computation.20.clone.1 | convolution fusion | flops 807010304 | bytes 3158021 | tf_op jit(solution)/shard_map/while/body/eval_jaxpr/dot_general | solution.py:87
  120.6 2.0 fusion.60
  122.7 0.3 fusion.61
  123.0 0.5 fusion.62
  123.5 3.7 %convolution_add_fusion.4 = f32[512,128]{1,0:T(8,128)} fusion(f32[2,1024,128]{2,1,0:T(8,128)S(1)} %get-tuple-element.467, s32[]{:T(128)} %get-tuple-element.453, f32[1024,512]{0,1:T(8,128)S(1)} %get-tuple-element.407, f32[1024]{0:T(1024)S(1)} %bitcast.77, f32[1024]{0:T(1024)S(1)} %fusion.61, f32[1024]{0:T(1024)S(1)} %get-tuple-element.408, ...), kind=kOutput, calls=%fused_computation.20.clone.1 | convolution fusion | flops 807010304 | bytes 3158021 | tf_op jit(solution)/shard_map/while/body/eval_jaxpr/dot_general | solution.py:87
  127.2 0.2 concatenate.66
  127.4 1.0 pad_maximum_fusion.2
  128.4 16.1 %all_to_all.33 = f32[32,16,129]{2,1,0:T(8,128)S(1)} all-to-all(f32[32,16,129]{2,1,0:T(8,128)S(1)} %pad_maximum_fusion.2), channel_id=1, replica_groups=mesh['grp'=8,'mem_0'=4,'mem_1'=4,'mem_2'=2] {'mem_0','mem_1','mem_2'}, dimensions={0} | all-to-all | bytes 528384 | tf_op jit(solution)/shard_map/all_to_all | solution.py:28
  144.7 0.7 broadcast_in_dim.9
  145.3 4.3 %all-to-all-start.3 = ((f32[8,1,2064]{2,1,0:T(1,128)}), f32[8,1,2064]{2,1,0:T(1,128)S(1)}, u32[]{:S(2)}, u32[]{:S(2)}) async-start(f32[8,1,2064]{2,1,0:T(1,128)} %broadcast_in_dim.9), calls=%async_computation.3 | async-start | bytes 139264 | tf_op jit(solution)/shard_map/all_to_all | solution.py:45
  149.6 7.2 %all-to-all-done.3 = f32[8,1,2064]{2,1,0:T(1,128)S(1)} async-done(((f32[8,1,2064]{2,1,0:T(1,128)}), f32[8,1,2064]{2,1,0:T(1,128)S(1)}, u32[]{:S(2)}, u32[]{:S(2)}) %all-to-all-start.3) | async-done | bytes 66080 | tf_op jit(solution)/shard_map/all_to_all | solution.py:45
  157.1 24.9 %all_gather.39 = f32[512,129]{1,0:T(8,128)S(1)} all-gather(f32[16,129]{1,0:T(8,128)S(1)} %pad_maximum_fusion.7), channel_id=1, replica_groups=mesh['grp'=8,'mem_0'=4,'mem_1'=4,'mem_2'=2] {'mem_0','mem_1','mem_2'}, dimensions={0}, use_global_device_ids=true | all-gather | bytes 272448 | tf_op jit(solution)/shard_map/all_gather | solution.py:65
  182.1 0.2 add_reduce_fusion
  182.6 12.3 %while.41 = (s32[]{:T(128)}, f32[512,128]{1,0:T(8,128)}, f32[512]{0:T(512)S(1)}, f32[512]{0:T(512)S(1)}, f32[2,1024,128]{2,1,0:T(8,128)S(1)}, /*index=5*/f32[512...) while((s32[]{:T(128)}, f32[512,128]{1,0:T(8,128)}, ...), condition=%wide.region_23.24_spmd.clone, body=%wide.region_19.23_spmd.clone.sunk | while | flops 1617559040 | bytes 10293372 | solution.py:101
  182.6 2.0 fusion.65
  184.7 0.3 fusion.66
  185.0 0.5 fusion.67
  185.5 2.7 %convolution_add_fusion.5 = f32[512,128]{1,0:T(8,128)} fusion(f32[2,1024,128]{2,1,0:T(8,128)S(1)} %get-tuple-element.497, s32[]{:T(128)} %get-tuple-element.483, f32[1024,512]{0,1:T(8,128)S(1)} %get-tuple-element.417, f32[1024]{0:T(1024)S(1)} %bitcast.80, f32[1024]{0:T(1024)S(1)} %fusion.66, f32[1024]{0:T(1024)S(1)} %get-tuple-element.418, ...), kind=kOutput, calls=%fused_computation.35.clone.1 | convolution fusion | flops 807010304 | bytes 3158021 | tf_op jit(solution)/shard_map/while/body/eval_jaxpr/dot_general | solution.py:87
  188.3 2.0 fusion.65
  190.3 0.3 fusion.66
  190.7 0.5 fusion.67
  191.2 3.7 %convolution_add_fusion.5 = f32[512,128]{1,0:T(8,128)} fusion(f32[2,1024,128]{2,1,0:T(8,128)S(1)} %get-tuple-element.497, s32[]{:T(128)} %get-tuple-element.483, f32[1024,512]{0,1:T(8,128)S(1)} %get-tuple-element.417, f32[1024]{0:T(1024)S(1)} %bitcast.80, f32[1024]{0:T(1024)S(1)} %fusion.66, f32[1024]{0:T(1024)S(1)} %get-tuple-element.418, ...), kind=kOutput, calls=%fused_computation.35.clone.1 | convolution fusion | flops 807010304 | bytes 3158021 | tf_op jit(solution)/shard_map/while/body/eval_jaxpr/dot_general | solution.py:87
  195.1 1.0 pad_maximum_fusion.3
  196.1 15.7 %all_to_all.34 = f32[32,16,129]{2,1,0:T(8,128)S(1)} all-to-all(f32[32,16,129]{2,1,0:T(8,128)S(1)} %pad_maximum_fusion.3), channel_id=1, replica_groups=mesh['grp'=8,'mem_0'=4,'mem_1'=4,'mem_2'=2] {'mem_0','mem_1','mem_2'}, dimensions={0} | all-to-all | bytes 528384 | tf_op jit(solution)/shard_map/all_to_all | solution.py:28
  212.0 9.6 %all_to_all.35 = f32[8,1,2064]{2,1,0:T(1,128)S(1)} all-to-all(f32[8,1,2064]{2,1,0:T(1,128)S(1)} %broadcast_in_dim.10), channel_id=1, replica_groups=mesh['grp'=8,'mem_0'=4,'mem_1'=4,'mem_2'=2] {'grp'}, dimensions={0} | all-to-all | bytes 132096 | tf_op jit(solution)/shard_map/all_to_all | solution.py:45
  221.6 0.5 broadcast_divide_fusion
  222.1 0.7 fusion.33
  (75 shorter events, 2.3 us)
Async XLA Ops:
  1.9 1.5 copy-start.1
  1.9 1.5 copy-start
  11.9 30.1 %copy-start.5 = (u32[256]{0:T(256)S(1)}, u32[256]{0:T(256)}, u32[]{:S(2)}) copy-start(u32[256]{0:T(256)} %constant.58) | copy-start | bytes 3076
  11.9 46.1 %copy-start.4 = (u32[256]{0:T(256)S(1)}, u32[256]{0:T(256)}, u32[]{:S(2)}) copy-start(u32[256]{0:T(256)} %constant.63) | copy-start | bytes 3076
  11.9 55.4 %copy-start.3 = (u32[256]{0:T(256)S(1)}, u32[256]{0:T(256)}, u32[]{:S(2)}) copy-start(u32[256]{0:T(256)} %constant.68) | copy-start | bytes 3076
  11.9 65.4 %copy-start.2 = (u32[256]{0:T(256)S(1)}, u32[256]{0:T(256)}, u32[]{:S(2)}) copy-start(u32[256]{0:T(256)} %constant.73) | copy-start | bytes 3076
  13.0 20.0 %all-to-all-start = ((f32[32,16,129]{2,1,0:T(8,128)}), f32[32,16,129]{2,1,0:T(8,128)S(1)}, u32[]{:S(2)}, u32[]{:S(2)}) async-start(f32[32,16,129]{2,1,0:T(8,128)} %pad_maximum_fusion.1), calls=%async_computation | async-start | bytes 1048576 | tf_op jit(solution)/shard_map/all_to_all | solution.py:28
  33.8 57.3 %all-to-all-start.1 = ((f32[8,1,2064]{2,1,0:T(1,128)}), f32[8,1,2064]{2,1,0:T(1,128)S(1)}, u32[]{:S(2)}, u32[]{:S(2)}) async-start(f32[8,1,2064]{2,1,0:T(1,128)} %broadcast_in_dim.8), calls=%async_computation.1 | async-start | bytes 139264 | tf_op jit(solution)/shard_map/all_to_all | solution.py:45
  145.3 11.5 %all-to-all-start.3 = ((f32[8,1,2064]{2,1,0:T(1,128)}), f32[8,1,2064]{2,1,0:T(1,128)S(1)}, u32[]{:S(2)}, u32[]{:S(2)}) async-start(f32[8,1,2064]{2,1,0:T(1,128)} %broadcast_in_dim.9), calls=%async_computation.3 | async-start | bytes 139264 | tf_op jit(solution)/shard_map/all_to_all | solution.py:45
